TPU v7x, 512 devices: a whole 4x4x16 slice. The times are simulated.
512 devices in a mesh: blk: 32 (over y, z_lo, core), replica: 16 (over z_hi, x).
Axes of the slice: x: 4, y: 4, z: 16 (z_hi: 4, z_lo: 4; z = z_hi * 4 + z_lo), core: 2. Of those that a mesh axis runs over, the one named last changes fastest.
Arguments:
- tokens: bfloat16 [640, 4096], P('blk', 'replica'), may hold values from -6 to 6
- cotangent: bfloat16 [640, 4096], P('blk', 'replica'), may hold values from -6 to 6
- gate_weight: bfloat16 [4096, 28672], P('replica', 'blk'), may hold values from -36 to 36, as said below
- up_weight: bfloat16 [4096, 28672], P('replica', 'blk'), may hold values from -36 to 36, as said below
- down_weight: bfloat16 [28672, 4096], P('blk', 'replica'), may hold values from -72 to 72, as said below
- gate_gain: float32 [28672], P('blk'), may hold values from 0.25 to 1.75
- up_gain: float32 [28672], P('blk'), may hold values from 0.25 to 1.75
- down_gain: float32 [4096], P('replica'), may hold values from 0.25 to 1.75
Outputs:
- grad_tokens: float32 [640, 4096], P('blk', 'replica')
- grad_gate: float32 [4096, 28672], P('replica', 'blk')
- grad_up: float32 [4096, 28672], P('replica', 'blk')
- grad_down: float32 [28672, 4096], P('blk', 'replica')
- grad_gate_gain: float32 [28672], P('blk')
- grad_up_gain: float32 [28672], P('blk')
- grad_down_gain: float32 [4096], P('replica')
Inputs may be any that keep to these rules, and one draw needn't show every extreme that they name: `gate_weight`: real-valued raw weights. `up_weight`: real-valued raw weights. `down_weight`: real-valued raw weights.
All inputs are finite; a program needn't handle non-finite values.
Results may differ from a plain program's by a relative error of at most 0.033.
Values may be sent and summed in bfloat16 or wider, within the bound.
No kernel may reach another device: no remote copies, remote signals or barrier semaphores. Data moves between devices by JAX's collectives and lax.ppermute only.
A program may use at most 64 MiB of HBM per device.

v0:
```python
import jax
import jax.numpy as jnp
from jax import lax
from jax.sharding import PartitionSpec as P

epsilon = 0.0001
branch_scale = 0.5


def sent_to_all(x, axis):
    copies = jnp.broadcast_to(x, (lax.axis_size(axis), *x.shape))
    return lax.all_to_all(copies, axis, split_axis=0, concat_axis=0, tiled=True)


def of_everyone(x, axis):
    return sent_to_all(x, axis).sum(axis=0)


def in_one(arrays, axis):
    ends = [0]
    for a in arrays:
        ends.append(ends[-1] + a.size)
    subtotal = of_everyone(jnp.concatenate([a.ravel() for a in arrays]), axis)
    return tuple((subtotal[b:e].reshape(a.shape) for a, b, e in zip(arrays, ends, ends[1:])))


def sent_together(arrays, axis, dim, along):
    both = jnp.concatenate(arrays, axis=along)
    result, at, done = (lax.all_gather(both, axis, axis=dim, tiled=True), 0, [])
    for a in arrays:
        done.append(lax.slice_in_dim(result, at, at + a.shape[along], axis=along))
        at += a.shape[along]
    return tuple(done)


def split_up(x, dim, devices):
    before, after = (x.shape[:dim], x.shape[dim + 1 :])
    return jnp.moveaxis(x.reshape(*before, devices, -1, *after), dim, 0)


def sum_at_owner(x, axis, dim):
    parts = split_up(x, dim, lax.axis_size(axis))
    arrived = lax.all_to_all(parts, axis, split_axis=0, concat_axis=0, tiled=True)
    return arrived.astype(jnp.float32).sum(axis=0)


def contract_first(left, right):
    return lax.dot_general(
        left, right, (((0,), (0,)), ((), ())), preferred_element_type=jnp.float32
    )


def contract_last(left, right):
    return lax.dot_general(
        left, right, (((1,), (1,)), ((), ())), preferred_element_type=jnp.float32
    )


def weight_grad(grad_hat, gain, cent, scale, summed, crossed, count):
    grad = scale * (gain * grad_hat - gain * summed / count) - scale * scale * scale * cent * (
        gain * crossed
    )
    return (grad, scale * crossed)


def gating(gate, up, dhidden):
    act = jax.nn.silu(gate)
    hidden = (act * up).astype(jnp.bfloat16)
    sig = jax.nn.sigmoid(gate)
    d_gate = (dhidden * up * sig * (1.0 + gate * (1.0 - sig))).astype(jnp.bfloat16)
    d_up = (dhidden * act).astype(jnp.bfloat16)
    return (d_gate, d_up, hidden)


def local(tokens, cotangent, gate_weight, up_weight, down_weight, gate_gain, up_gain, down_gain):
    width_all = gate_weight.shape[0] * lax.axis_size("replica")
    hidden_all = down_weight.shape[0] * lax.axis_size("blk")
    gate_raw = gate_weight.astype(jnp.float32)
    up_raw = up_weight.astype(jnp.float32)
    down_raw = down_weight.astype(jnp.float32)
    gate_sum, gate_power, up_sum, up_power = in_one(
        (
            jnp.sum(gate_raw, axis=0),
            jnp.sum(gate_raw * gate_raw, axis=0),
            jnp.sum(up_raw, axis=0),
            jnp.sum(up_raw * up_raw, axis=0),
        ),
        "replica",
    )
    gate_mean = gate_sum / width_all
    up_mean = up_sum / width_all
    gate_cent = gate_raw - gate_mean
    up_cent = up_raw - up_mean
    gate_square = gate_power - gate_sum * gate_mean
    up_square = up_power - up_sum * up_mean
    down_sum, down_power = in_one(
        (jnp.sum(down_raw, axis=0), jnp.sum(down_raw * down_raw, axis=0)), "blk"
    )
    down_mean = down_sum / hidden_all
    down_cent = down_raw - down_mean
    down_square = down_power - down_sum * down_mean
    gate_scale = lax.rsqrt(gate_square + epsilon)
    up_scale = lax.rsqrt(up_square + epsilon)
    down_scale = lax.rsqrt(down_square + epsilon)
    gate_hat = (gate_gain * gate_cent * gate_scale).astype(jnp.bfloat16)
    up_hat = (up_gain * up_cent * up_scale).astype(jnp.bfloat16)
    down_hat = (down_gain * down_cent * down_scale).astype(jnp.bfloat16)
    scaled = (branch_scale * cotangent.astype(jnp.float32)).astype(jnp.bfloat16)
    whole_tokens, whole_scaled = sent_together((tokens, scaled), "blk", 0, 1)
    gate_part = jnp.dot(whole_tokens, gate_hat, preferred_element_type=jnp.float32).astype(
        jnp.bfloat16
    )
    up_part = jnp.dot(whole_tokens, up_hat, preferred_element_type=jnp.float32).astype(jnp.bfloat16)
    down_part = contract_last(whole_scaled, down_hat).astype(jnp.bfloat16)
    gate, up, dhidden = (
        lax.psum(gate_part, "replica").astype(jnp.float32),
        lax.psum(up_part, "replica").astype(jnp.float32),
        lax.psum(down_part, "replica").astype(jnp.float32),
    )
    d_gate, d_up, hidden = gating(gate, up, dhidden)
    share = sum_at_owner(
        (contract_last(d_gate, gate_hat) + contract_last(d_up, up_hat)).astype(jnp.bfloat16),
        "blk",
        0,
    )
    grad_tokens = cotangent.astype(jnp.float32) + share
    p_gate = contract_first(whole_tokens, d_gate)
    p_up = contract_first(whole_tokens, d_up)
    p_down = contract_first(hidden, whole_scaled)
    gate_psum, gate_pcross, up_psum, up_pcross = in_one(
        (
            jnp.sum(p_gate, axis=0),
            jnp.sum(p_gate * gate_cent, axis=0),
            jnp.sum(p_up, axis=0),
            jnp.sum(p_up * up_cent, axis=0),
        ),
        "replica",
    )
    down_psum, down_pcross = in_one(
        (jnp.sum(p_down, axis=0), jnp.sum(p_down * down_cent, axis=0)), "blk"
    )
    grad_gate, grad_gate_gain = weight_grad(
        p_gate, gate_gain, gate_cent, gate_scale, gate_psum, gate_pcross, width_all
    )
    grad_up, grad_up_gain = weight_grad(
        p_up, up_gain, up_cent, up_scale, up_psum, up_pcross, width_all
    )
    grad_down, grad_down_gain = weight_grad(
        p_down, down_gain, down_cent, down_scale, down_psum, down_pcross, hidden_all
    )
    return (
        grad_tokens,
        grad_gate,
        grad_up,
        grad_down,
        grad_gate_gain,
        grad_up_gain,
        grad_down_gain,
    )


def solution(mesh):
    return jax.shard_map(
        local,
        mesh=mesh,
        in_specs=(
            P("blk", "replica"),
            P("blk", "replica"),
            P("replica", "blk"),
            P("replica", "blk"),
            P("blk", "replica"),
            P("blk"),
            P("blk"),
            P("replica"),
        ),
        out_specs=(
            P("blk", "replica"),
            P("replica", "blk"),
            P("replica", "blk"),
            P("blk", "replica"),
            P("blk"),
            P("blk"),
            P("replica"),
        ),
        check_vma=False,
    )
```

profile of v0, /device:TPU:1, one launch (start us, length us, event | category | flops | bytes accessed | tf_op | source)
XLA Modules:
  0.0 533.1 jit_solution(5313933197506070054)
XLA Ops:
  7.2 1.2 convert_reduce_fusion.2
  8.4 0.7 broadcast_in_dim.8
  9.1 10.3 %all-to-all-start = ((f32[32,1,512]{2,1,0:T(1,128)}), f32[32,1,512]{2,1,0:T(1,128)S(1)}, u32[]{:S(2)}, u32[]{:S(2)}) async-start(f32[32,1,512]{2,1,0:T(1,128)} %broadcast_in_dim.8), calls=%async_computation | async-start | bytes 131072 | tf_op jit(solution)/shard_map/all_to_all | solution.py:12
  19.4 1.4 convert_reduce_fusion
  20.9 6.4 %all-to-all-done = f32[32,1,512]{2,1,0:T(1,128)S(1)} async-done(((f32[32,1,512]{2,1,0:T(1,128)}), f32[32,1,512]{2,1,0:T(1,128)S(1)}, u32[]{:S(2)}, u32[]{:S(2)}) %all-to-all-start) | async-done | bytes 65568 | tf_op jit(solution)/shard_map/all_to_all | solution.py:12
  27.3 0.8 broadcast_in_dim.9
  28.1 14.4 %all-to-all-start.1 = ((f32[16,1,3584]{2,1,0:T(1,128)}), f32[16,1,3584]{2,1,0:T(1,128)S(1)}, u32[]{:S(2)}, u32[]{:S(2)}) async-start(f32[16,1,3584]{2,1,0:T(1,128)} %broadcast_in_dim.9), calls=%async_computation.1 | async-start | bytes 458752 | tf_op jit(solution)/shard_map/all_to_all | solution.py:12
  42.6 46.4 %all-gather = bf16[32,20,512]{2,1,0:T(8,128)(2,1)S(1)} all-gather(bf16[1,20,512]{2,1,0:T(8,128)(2,1)S(1)} %maximum_bitcast_fusion), channel_id=1, replica_groups=mesh['blk'=32,'replica'=16] {'blk'}, dimensions={0}, use_global_device_ids=true | all-gather | bytes 675840 | tf_op jit(solution)/shard_map/all_gather | solution.py:29
  89.2 0.7 multiply_multiply_fusion.2
  89.9 1.6 convolution_convert_fusion.2
  92.3 1.6 convolution_convert_fusion
  93.9 1.6 convolution_convert_fusion.1
  95.5 358.5 %all-reduce.3.cloned.1.call-done = (bf16[640,896]{1,0:T(8,128)(2,1)}, bf16[640,896]{1,0:T(8,128)(2,1)}, bf16[640,896]{1,0:T(8,128)(2,1)}) async-done(((bf16[640,896]{1,0:T(8,128)(2,1)}, bf16[640,896]{1,0:T(8,128)(2,1)}, bf16[640,896]{1,0:T(8,128)(2,1)}), (bf16[640,896]{1,0:T(8,128)(2,1)}, bf16[640,896]{1,0:T(8,128)(2,1)}, bf16[640,896]{1,0:T(8,128)(2,1)})) %all-reduce.3.cloned.1.call-update) | async-done | bytes 3440656 | tf_op jit(solution)/shard_map/psum | solution.py:117
  454.1 3.7 fusion.64
  457.7 2.3 fusion
  460.0 0.7 broadcast_in_dim.11
  460.7 6.7 %all-to-all-start.4 = ((f32[32,1,512]{2,1,0:T(1,128)}), f32[32,1,512]{2,1,0:T(1,128)S(1)}, u32[]{:S(2)}, u32[]{:S(2)}) async-start(f32[32,1,512]{2,1,0:T(1,128)} %broadcast_in_dim.11), calls=%async_computation.4 | async-start | bytes 131072 | tf_op jit(solution)/shard_map/all_to_all | solution.py:12
  467.4 1.7 fusion.66
  469.2 1.5 fusion.65
  470.7 4.5 all-to-all-done.4
  475.2 0.8 broadcast_in_dim.10
  476.0 10.2 %all-to-all-start.3 = ((f32[16,1,3584]{2,1,0:T(1,128)}), f32[16,1,3584]{2,1,0:T(1,128)}, u32[]{:S(2)}, u32[]{:S(2)}) async-start(f32[16,1,3584]{2,1,0:T(1,128)} %broadcast_in_dim.10), calls=%async_computation.3 | async-start | bytes 458752 | tf_op jit(solution)/shard_map/all_to_all | solution.py:12
  486.2 1.8 fusion.45
  488.0 1.3 fusion.18
  489.3 1.8 reshape.51
  491.2 11.7 %all-to-all-done.3 = f32[16,1,3584]{2,1,0:T(1,128)} async-done(((f32[16,1,3584]{2,1,0:T(1,128)}), f32[16,1,3584]{2,1,0:T(1,128)}, u32[]{:S(2)}, u32[]{:S(2)}) %all-to-all-start.3) | async-done | bytes 229408 | tf_op jit(solution)/shard_map/all_to_all | solution.py:12
  502.9 8.6 %all-to-all-start.2 = ((bf16[32,20,256]{2,1,0:T(8,128)(2,1)}), bf16[32,20,256]{2,1,0:T(8,128)(2,1)S(1)}, u32[]{:S(2)}, u32[]{:S(2)}) async-start(bf16[32,20,256]{2,1,0:T(8,128)(2,1)} %reshape.51), calls=%async_computation.2 | async-start | bytes 786432 | tf_op jit(solution)/shard_map/all_to_all | solution.py:43
  512.1 2.4 fusion.35
  514.5 1.1 reduce_sum.166
  516.2 2.3 fusion.25
  518.5 1.2 fusion.30
  519.7 5.8 %all-to-all-done.2 = bf16[32,20,256]{2,1,0:T(8,128)(2,1)S(1)} async-done(((bf16[32,20,256]{2,1,0:T(8,128)(2,1)}), bf16[32,20,256]{2,1,0:T(8,128)(2,1)S(1)}, u32[]{:S(2)}, u32[]{:S(2)}) %all-to-all-start.2) | async-done | bytes 327712 | tf_op jit(solution)/shard_map/all_to_all | solution.py:43
  (68 shorter events, 3.1 us)
Async XLA Ops:
  7.2 13.7 %copy-start.9 = (bf16[20,256]{1,0:T(8,128)(2,1)S(1)}, bf16[20,256]{1,0:T(8,128)(2,1)}, u32[]{:S(2)}) copy-start(bf16[20,256]{1,0:T(8,128)(2,1)} %param.9) | copy-start | bytes 30724
  7.2 35.4 %copy-start.17 = (bf16[20,256]{1,0:T(8,128)(2,1)S(1)}, bf16[20,256]{1,0:T(8,128)(2,1)}, u32[]{:S(2)}) copy-start(bf16[20,256]{1,0:T(8,128)(2,1)} %param.8) | copy-start | bytes 30724
  9.1 18.2 %all-to-all-start = ((f32[32,1,512]{2,1,0:T(1,128)}), f32[32,1,512]{2,1,0:T(1,128)S(1)}, u32[]{:S(2)}, u32[]{:S(2)}) async-start(f32[32,1,512]{2,1,0:T(1,128)} %broadcast_in_dim.8), calls=%async_computation | async-start | bytes 131072 | tf_op jit(solution)/shard_map/all_to_all | solution.py:12
  28.1 63.4 %all-to-all-start.1 = ((f32[16,1,3584]{2,1,0:T(1,128)}), f32[16,1,3584]{2,1,0:T(1,128)S(1)}, u32[]{:S(2)}, u32[]{:S(2)}) async-start(f32[16,1,3584]{2,1,0:T(1,128)} %broadcast_in_dim.9), calls=%async_computation.1 | async-start | bytes 458752 | tf_op jit(solution)/shard_map/all_to_all | solution.py:12
  42.5 411.5 %all-reduce.3.cloned.1.call-start = ((), (), s32[]{:S(2)}) async-start(), calls=%async_computation.5 | async-start | bytes 6881280 | tf_op jit(solution)/shard_map/psum | solution.py:117
  42.6 47.3 %copy-start = (bf16[896,256]{1,0:T(8,128)(2,1)S(1)}, bf16[896,256]{1,0:T(8,128)(2,1)}, u32[]{:S(2)}) copy-start(bf16[896,256]{1,0:T(8,128)(2,1)} %param.12) | copy-start | bytes 1376260
  42.6 47.3 %copy-start.20 = (f32[256]{0:T(256)S(1)}, f32[256]{0:T(256)}, u32[]{:S(2)}) copy-start(f32[256]{0:T(256)} %param.15) | copy-start | bytes 3076
  89.1 364.9 %copy-start.7 = (bf16[640,512]{1,0:T(8,128)(2,1)}, bf16[640,512]{1,0:T(8,128)(2,1)S(1)}, u32[]{:S(2)}) copy-start(bf16[640,512]{1,0:T(8,128)(2,1)S(1)} %reshape.53) | copy-start | bytes 1966084
  89.9 1.6 copy-start.18
  89.9 364.2 %copy-start.23 = (f32[256]{0:T(256)}, f32[256]{0:T(256)S(1)}, u32[]{:S(2)}) copy-start(f32[256]{0:T(256)S(1)} %get-tuple-element.46) | copy-start | bytes 3076
  89.9 2.4 copy-start.1
  89.9 2.4 copy-start.10
  91.5 2.4 copy-start.2
  91.5 2.4 copy-start.11
  92.3 375.1 %copy-start.12 = (f32[896]{0:T(1024)}, f32[896]{0:T(1024)S(1)}, u32[]{:S(2)}) copy-start(f32[896]{0:T(1024)S(1)} %get-tuple-element.42) | copy-start | bytes 10756
  92.3 376.9 %copy-start.15 = (f32[896]{0:T(1024)}, f32[896]{0:T(1024)S(1)}, u32[]{:S(2)}) copy-start(f32[896]{0:T(1024)S(1)} %get-tuple-element.39) | copy-start | bytes 10756
  454.0 3.7 copy-start.4
  454.1 3.7 copy-start.5
  454.1 3.7 copy-start.6
  460.7 14.5 %all-to-all-start.4 = ((f32[32,1,512]{2,1,0:T(1,128)}), f32[32,1,512]{2,1,0:T(1,128)S(1)}, u32[]{:S(2)}, u32[]{:S(2)}) async-start(f32[32,1,512]{2,1,0:T(1,128)} %broadcast_in_dim.11), calls=%async_computation.4 | async-start | bytes 131072 | tf_op jit(solution)/shard_map/all_to_all | solution.py:12
  467.4 1.7 copy-start.3
  467.4 1.7 copy-start.8
  476.0 26.9 %all-to-all-start.3 = ((f32[16,1,3584]{2,1,0:T(1,128)}), f32[16,1,3584]{2,1,0:T(1,128)}, u32[]{:S(2)}, u32[]{:S(2)}) async-start(f32[16,1,3584]{2,1,0:T(1,128)} %broadcast_in_dim.10), calls=%async_computation.3 | async-start | bytes 458752 | tf_op jit(solution)/shard_map/all_to_all | solution.py:12
  486.2 1.8 copy-start.13
  489.3 22.2 %copy-start.19 = (f32[256]{0:T(256)S(1)}, f32[256]{0:T(256)}, u32[]{:S(2)}) copy-start(f32[256]{0:T(256)} %copy-done.18) | copy-start | bytes 3076
  489.3 22.2 %copy-start.21 = (f32[256]{0:T(256)S(1)}, f32[256]{0:T(256)}, u32[]{:S(2)}) copy-start(f32[256]{0:T(256)} %param.15) | copy-start | bytes 3076
  489.3 22.8 %copy-start.22 = (f32[256]{0:T(256)S(1)}, f32[256]{0:T(256)}, u32[]{:S(2)}) copy-start(f32[256]{0:T(256)} %get-tuple-element.22) | copy-start | bytes 3076
  489.3 22.8 %copy-start.24 = (f32[256]{0:T(256)S(1)}, f32[256]{0:T(256)}, u32[]{:S(2)}) copy-start(f32[256]{0:T(256)} %copy-done.23) | copy-start | bytes 3076
  502.9 22.7 %all-to-all-start.2 = ((bf16[32,20,256]{2,1,0:T(8,128)(2,1)}), bf16[32,20,256]{2,1,0:T(8,128)(2,1)S(1)}, u32[]{:S(2)}, u32[]{:S(2)}) async-start(bf16[32,20,256]{2,1,0:T(8,128)(2,1)} %reshape.51), calls=%async_computation.2 | async-start | bytes 786432 | tf_op jit(solution)/shard_map/all_to_all | solution.py:43
  512.1 4.1 copy-start.14
  512.1 4.1 copy-start.16
Sparse Core Ops, SparseCore 0:
  95.6 358.3 all-reduce.2
where the time goes:
time: 534 us; the launch traced here: 533 us
  waiting for transfers between devices  387 us (72%)
  starting transfers between devices  50.3 us (9%)
  blocking collectives  46.4 us (9%)
  other arithmetic  15.3 us (3%)
  matrix products  14.7 us (3%)
  between operations  14.3 us (3%)
    psum x1, waiting for transfers between devices, local(): lax.psum(up_part, 'replica').astype(jnp.float32)  359 us
    all_gather x1, blocking collectives, sent_together(): result, at, done = (lax.all_gather(both, axis, axis=dim, tiled=True), 0, [])  46.4 us
    all_to_all x4, starting transfers between devices, sent_to_all(): return lax.all_to_all(copies, axis, split_axis=0, concat_axis=0, tiled=True)  41.6 us
    all_to_all x4, waiting for transfers between devices, sent_to_all(): return lax.all_to_all(copies, axis, split_axis=0, concat_axis=0, tiled=True)  22.6 us
  transfers between devices with their start and end apart: 6, of which 5 were waited for; matrix products, arithmetic and copies ran while one was open for 4% of the time, Pallas kernels for 0%

commit v1 on v0

--- a/solution.py
+++ b/solution.py
@@ -5,6 +5,12 @@
 
 epsilon = 0.0001
 branch_scale = 0.5
+
+
+def summed_here(x, mesh_axis):
+    parts = lax.all_gather(x, mesh_axis, axis=0, tiled=False)
+    result = parts.sum(axis=0)
+    return result
 
 
 def sent_to_all(x, axis):
@@ -114,7 +120,7 @@
     down_part = contract_last(whole_scaled, down_hat).astype(jnp.bfloat16)
     gate, up, dhidden = (
         lax.psum(gate_part, "replica").astype(jnp.float32),
-        lax.psum(up_part, "replica").astype(jnp.float32),
+        summed_here(up_part, "replica").astype(jnp.float32),
         lax.psum(down_part, "replica").astype(jnp.float32),
     )
     d_gate, d_up, hidden = gating(gate, up, dhidden)

time: 534 us -> 852 us (1.60)
  waiting for transfers between devices: 387 us -> 683 us
  blocking collectives: 46.4 us -> 59.9 us
  other arithmetic: 15.3 us -> 24.6 us
    all_gather x0 -> x1, waiting for transfers between devices: none -> 400 us  [summed_here(): parts = lax.all_gather(x, mesh_axis, axis=0, tiled=False)]
    psum x1, waiting for transfers between devices: 359 us -> 259 us  [local(): lax.psum(down_part, 'replica').astype(jnp.float32)]
    all_to_all x0 -> x1, blocking collectives: none -> 10.8 us  [sent_to_all(): return lax.all_to_all(copies, axis, split_axis=0, concat_axis=0, tiled=True)]
    reduce_sum x0 -> x1, other arithmetic: none -> 9.98 us  [summed_here(): result = parts.sum(axis=0)]
    all_to_all x4 -> x3, waiting for transfers between devices: 22.6 us -> 18.1 us  [sent_to_all(): return lax.all_to_all(copies, axis, split_axis=0, concat_axis=0, tiled=True)]
    all_to_all x4 -> x3, starting transfers between devices: 41.6 us -> 44 us  [sent_to_all(): return lax.all_to_all(copies, axis, split_axis=0, concat_axis=0, tiled=True)]
  transfers between devices with their start and end apart: 6 -> 6, of which waited for: 5 -> 5; matrix products, arithmetic and copies ran while one was open for 4% -> 3% of each run, Pallas kernels for 0% -> 0%
where the time goes in v1:
time: 852 us
  waiting for transfers between devices  683 us (80%)
  blocking collectives  59.9 us (7%)
  starting transfers between devices  53 us (6%)
  other arithmetic  24.6 us (3%)
  between operations  14.4 us (2%)
  matrix products  13.5 us (2%)
    all_gather x1, waiting for transfers between devices, summed_here(): parts = lax.all_gather(x, mesh_axis, axis=0, tiled=False)  400 us
    psum x1, waiting for transfers between devices, local(): lax.psum(down_part, 'replica').astype(jnp.float32)  259 us
    all_gather x1, blocking collectives, sent_together(): result, at, done = (lax.all_gather(both, axis, axis=dim, tiled=True), 0, [])  49.1 us
    all_to_all x3, starting transfers between devices, sent_to_all(): return lax.all_to_all(copies, axis, split_axis=0, concat_axis=0, tiled=True)  44 us
    all_to_all x3, waiting for transfers between devices, sent_to_all(): return lax.all_to_all(copies, axis, split_axis=0, concat_axis=0, tiled=True)  18.1 us
  transfers between devices with their start and end apart: 6, of which 5 were waited for; matrix products, arithmetic and copies ran while one was open for 3% of the time, Pallas kernels for 0%

profile of v1, /device:TPU:1, one launch (start us, length us, event | category | flops | bytes accessed | tf_op | source)
XLA Modules:
  0.0 851.7 jit_solution(8520168053173441434)
XLA Ops:
  7.2 1.4 convert_reduce_fusion
  8.6 0.8 broadcast_in_dim.9
  9.4 18.2 %all-to-all-start.1 = ((f32[16,1,3584]{2,1,0:T(1,128)}), f32[16,1,3584]{2,1,0:T(1,128)S(1)}, u32[]{:S(2)}, u32[]{:S(2)}) async-start(f32[16,1,3584]{2,1,0:T(1,128)} %broadcast_in_dim.9), calls=%async_computation.1 | async-start | bytes 458752 | tf_op jit(solution)/shard_map/all_to_all | solution.py:18
  27.8 49.1 %all-gather.1 = bf16[32,20,512]{2,1,0:T(8,128)(2,1)S(1)} all-gather(bf16[1,20,512]{2,1,0:T(8,128)(2,1)S(1)} %maximum_bitcast_fusion), channel_id=1, replica_groups=mesh['blk'=32,'replica'=16] {'blk'}, dimensions={0}, use_global_device_ids=true | all-gather | bytes 675840 | tf_op jit(solution)/shard_map/all_gather | solution.py:35
  77.2 0.6 multiply_multiply_fusion.1
  77.9 1.6 convolution_convert_fusion.1
  79.7 10.8 %all_to_all.29 = f32[32,1,512]{2,1,0:T(1,128)S(1)} all-to-all(f32[32,1,512]{2,1,0:T(1,128)S(1)} %broadcast_in_dim.8), channel_id=1, replica_groups=mesh['blk'=32,'replica'=16] {'blk'}, dimensions={0} | all-to-all | bytes 131072 | tf_op jit(solution)/shard_map/all_to_all | solution.py:18
  91.2 1.6 convolution_convert_fusion.2
  92.8 1.6 convolution_convert_fusion
  94.4 399.8 %all-gather.4.cloned.1.call-done = bf16[10240,896]{1,0:T(8,128)(2,1)} async-done(((bf16[640,896]{1,0:T(8,128)(2,1)}), bf16[10240,896]{1,0:T(8,128)(2,1)}) %all-gather.4.cloned.1.call-update) | async-done | bytes 18350096 | tf_op jit(solution)/shard_map/all_gather | solution.py:11
  494.2 10.0 %reduce_sum.173 = bf16[640,896]{1,0:T(8,128)(2,1)S(1)} reduce(bf16[16,640,896]{2,1,0:T(8,128)(2,1)} %bitcast.7, bf16[]{:T(256)} %constant.21.clone.1), dimensions={0}, to_apply=%region_9.0 | reduce | flops 8601600 | bytes 19496962 | tf_op jit(solution)/shard_map/reduce_sum | solution.py:12
  504.2 259.2 %all-reduce.3.cloned.1.call-done = (bf16[640,896]{1,0:T(8,128)(2,1)}, bf16[640,896]{1,0:T(8,128)(2,1)}) async-done(((bf16[640,896]{1,0:T(8,128)(2,1)}, bf16[640,896]{1,0:T(8,128)(2,1)}), (bf16[640,896]{1,0:T(8,128)(2,1)}, bf16[640,896]{1,0:T(8,128)(2,1)})) %all-reduce.3.cloned.1.call-update) | async-done | bytes 2293776 | tf_op jit(solution)/shard_map/psum | solution.py:124
  763.4 3.3 fusion.64
  766.7 2.7 fusion
  769.4 0.7 broadcast_in_dim.11
  770.0 14.2 %all-to-all-start.4 = ((f32[32,1,512]{2,1,0:T(1,128)}), f32[32,1,512]{2,1,0:T(1,128)S(1)}, u32[]{:S(2)}, u32[]{:S(2)}) async-start(f32[32,1,512]{2,1,0:T(1,128)} %broadcast_in_dim.11), calls=%async_computation.4 | async-start | bytes 131072 | tf_op jit(solution)/shard_map/all_to_all | solution.py:18
  784.3 2.1 fusion.66
  786.4 1.5 fusion.65
  787.9 4.2 all-to-all-done.4
  792.2 0.8 broadcast_in_dim.10
  793.0 11.6 %all-to-all-start.3 = ((f32[16,1,3584]{2,1,0:T(1,128)}), f32[16,1,3584]{2,1,0:T(1,128)}, u32[]{:S(2)}, u32[]{:S(2)}) async-start(f32[16,1,3584]{2,1,0:T(1,128)} %broadcast_in_dim.10), calls=%async_computation.3 | async-start | bytes 458752 | tf_op jit(solution)/shard_map/all_to_all | solution.py:18
  804.6 1.3 fusion.45
  806.6 0.8 reshape.51
  807.4 13.8 %all-to-all-done.3 = f32[16,1,3584]{2,1,0:T(1,128)} async-done(((f32[16,1,3584]{2,1,0:T(1,128)}), f32[16,1,3584]{2,1,0:T(1,128)}, u32[]{:S(2)}, u32[]{:S(2)}) %all-to-all-start.3) | async-done | bytes 229408 | tf_op jit(solution)/shard_map/all_to_all | solution.py:18
  821.3 8.9 %all-to-all-start.2 = ((bf16[32,20,256]{2,1,0:T(8,128)(2,1)}), bf16[32,20,256]{2,1,0:T(8,128)(2,1)S(1)}, u32[]{:S(2)}, u32[]{:S(2)}) async-start(bf16[32,20,256]{2,1,0:T(8,128)(2,1)} %reshape.51), calls=%async_computation.2 | async-start | bytes 786432 | tf_op jit(solution)/shard_map/all_to_all | solution.py:49
  830.8 2.4 fusion.35
  833.2 1.1 reduce_sum.179
  834.3 0.6 fusion.57
  834.9 2.3 fusion.25
  837.2 1.2 fusion.30
  838.4 5.8 all-to-all-done.2
  844.3 0.6 convert_add_fusion
  (71 shorter events, 2.7 us)
Async XLA Ops:
  7.2 20.5 %copy-start.9 = (bf16[20,256]{1,0:T(8,128)(2,1)S(1)}, bf16[20,256]{1,0:T(8,128)(2,1)}, u32[]{:S(2)}) copy-start(bf16[20,256]{1,0:T(8,128)(2,1)} %param.9) | copy-start | bytes 30724
  7.2 20.5 %copy-start.17 = (bf16[20,256]{1,0:T(8,128)(2,1)S(1)}, bf16[20,256]{1,0:T(8,128)(2,1)}, u32[]{:S(2)}) copy-start(bf16[20,256]{1,0:T(8,128)(2,1)} %param.8) | copy-start | bytes 30724
  9.4 67.6 %all-to-all-start.1 = ((f32[16,1,3584]{2,1,0:T(1,128)}), f32[16,1,3584]{2,1,0:T(1,128)S(1)}, u32[]{:S(2)}, u32[]{:S(2)}) async-start(f32[16,1,3584]{2,1,0:T(1,128)} %broadcast_in_dim.9), calls=%async_computation.1 | async-start | bytes 458752 | tf_op jit(solution)/shard_map/all_to_all | solution.py:18
  27.6 466.5 %all-gather.4.cloned.1.call-start = ((), (), s32[]{:S(2)}) async-start(), calls=%async_computation.5 | async-start | bytes 19496960 | tf_op jit(solution)/shard_map/all_gather | solution.py:11
  27.7 50.1 %copy-start.2 = (bf16[256,896]{1,0:T(8,128)(2,1)S(1)}, bf16[256,896]{1,0:T(8,128)(2,1)}, u32[]{:S(2)}) copy-start(bf16[256,896]{1,0:T(8,128)(2,1)} %param.11) | copy-start | bytes 1376260
  27.8 50.1 %copy-start.11 = (f32[896]{0:T(1024)S(1)}, f32[896]{0:T(1024)}, u32[]{:S(2)}) copy-start(f32[896]{0:T(1024)} %param.14) | copy-start | bytes 10756
  77.0 686.4 %copy-start.7 = (bf16[640,512]{1,0:T(8,128)(2,1)}, bf16[640,512]{1,0:T(8,128)(2,1)S(1)}, u32[]{:S(2)}) copy-start(bf16[640,512]{1,0:T(8,128)(2,1)S(1)} %reshape.54) | copy-start | bytes 1966084
  77.8 706.4 %copy-start.12 = (f32[896]{0:T(1024)}, f32[896]{0:T(1024)S(1)}, u32[]{:S(2)}) copy-start(f32[896]{0:T(1024)S(1)} %get-tuple-element.41) | copy-start | bytes 10756
  77.8 708.6 %copy-start.15 = (f32[896]{0:T(1024)}, f32[896]{0:T(1024)S(1)}, u32[]{:S(2)}) copy-start(f32[896]{0:T(1024)S(1)} %get-tuple-element.38) | copy-start | bytes 10756
  77.8 1.6 copy-start
  79.4 11.8 %copy-start.20 = (f32[256]{0:T(256)S(1)}, f32[256]{0:T(256)}, u32[]{:S(2)}) copy-start(f32[256]{0:T(256)} %param.15) | copy-start | bytes 3076
  79.4 683.9 %all-reduce.3.cloned.1.call-start = ((), (), s32[]{:S(2)}) async-start(), calls=%async_computation.6 | async-start | bytes 4587520 | tf_op jit(solution)/shard_map/psum | solution.py:124
  79.7 13.1 %copy-start.1 = (bf16[256,896]{1,0:T(8,128)(2,1)S(1)}, bf16[256,896]{1,0:T(8,128)(2,1)}, u32[]{:S(2)}) copy-start(bf16[256,896]{1,0:T(8,128)(2,1)} %param.10) | copy-start | bytes 1376260
  79.7 13.1 %copy-start.10 = (f32[896]{0:T(1024)S(1)}, f32[896]{0:T(1024)}, u32[]{:S(2)}) copy-start(f32[896]{0:T(1024)} %param.13) | copy-start | bytes 10756
  91.2 3.2 copy-start.18
  91.2 672.2 %copy-start.23 = (f32[256]{0:T(256)}, f32[256]{0:T(256)S(1)}, u32[]{:S(2)}) copy-start(f32[256]{0:T(256)S(1)} %get-tuple-element.45) | copy-start | bytes 3076
  763.4 3.3 copy-start.5
  763.4 3.3 copy-start.6
  770.0 22.1 %all-to-all-start.4 = ((f32[32,1,512]{2,1,0:T(1,128)}), f32[32,1,512]{2,1,0:T(1,128)S(1)}, u32[]{:S(2)}, u32[]{:S(2)}) async-start(f32[32,1,512]{2,1,0:T(1,128)} %broadcast_in_dim.11), calls=%async_computation.4 | async-start | bytes 131072 | tf_op jit(solution)/shard_map/all_to_all | solution.py:18
  784.3 2.1 copy-start.4
  784.3 2.1 copy-start.8
  793.0 28.3 %all-to-all-start.3 = ((f32[16,1,3584]{2,1,0:T(1,128)}), f32[16,1,3584]{2,1,0:T(1,128)}, u32[]{:S(2)}, u32[]{:S(2)}) async-start(f32[16,1,3584]{2,1,0:T(1,128)} %broadcast_in_dim.10), calls=%async_computation.3 | async-start | bytes 458752 | tf_op jit(solution)/shard_map/all_to_all | solution.py:18
  804.6 1.4 copy-start.3
  804.6 1.4 copy-start.13
  806.5 23.7 %copy-start.19 = (f32[256]{0:T(256)S(1)}, f32[256]{0:T(256)}, u32[]{:S(2)}) copy-start(f32[256]{0:T(256)} %copy-done.18) | copy-start | bytes 3076
  806.5 23.7 %copy-start.21 = (f32[256]{0:T(256)S(1)}, f32[256]{0:T(256)}, u32[]{:S(2)}) copy-start(f32[256]{0:T(256)} %param.15) | copy-start | bytes 3076
  806.6 24.2 %copy-start.22 = (f32[256]{0:T(256)S(1)}, f32[256]{0:T(256)}, u32[]{:S(2)}) copy-start(f32[256]{0:T(256)} %get-tuple-element.21) | copy-start | bytes 3076
  806.6 24.2 %copy-start.24 = (f32[256]{0:T(256)S(1)}, f32[256]{0:T(256)}, u32[]{:S(2)}) copy-start(f32[256]{0:T(256)} %copy-done.23) | copy-start | bytes 3076
  821.3 22.9 %all-to-all-start.2 = ((bf16[32,20,256]{2,1,0:T(8,128)(2,1)}), bf16[32,20,256]{2,1,0:T(8,128)(2,1)S(1)}, u32[]{:S(2)}, u32[]{:S(2)}) async-start(bf16[32,20,256]{2,1,0:T(8,128)(2,1)} %reshape.51), calls=%async_computation.2 | async-start | bytes 786432 | tf_op jit(solution)/shard_map/all_to_all | solution.py:49
  830.8 4.1 copy-start.14
  830.8 4.1 copy-start.16
Sparse Core Ops, SparseCore 0:
  79.6 414.5 all-gather.3
  497.2 266.1 all-reduce.2
